TPU v7x, 32 devices: a whole 2x2x4 slice. The times are simulated.
32 devices in a mesh: cls: 16 (over z, y, x), rep: 2 (over core).
Axes of the slice: x: 2, y: 2, z: 4, core: 2. Of those that a mesh axis runs over, the one named last changes fastest.
Arguments:
- queries: bfloat16 [2, 32, 768], P('rep', 'cls'), may hold values from -16 to 16
- positives: int32 [2, 32, 4], replicated, may hold values from -1 to 98303, as said below
- label_vectors: bfloat16 [98304, 768], P('cls'), may hold values from -80 to 80
- refresh_slot: int32 [], replicated, may hold values from 0 to 7
- features: bfloat16 [12288, 768], P(('cls', 'rep')), may hold values from -6 to 6
- encoder_weight: bfloat16 [768, 768], replicated, may hold values from -0.21875 to 0.21875
- encoder_gain: float32 [768], replicated, may hold values from 0.1 to 1.9
- free_vectors: bfloat16 [12288, 768], P(('cls', 'rep')), may hold values from -3 to 3
- targets: int32 [12288], replicated, may hold values from 0 to 12287, as said below
Outputs:
- loss: float32 [2, 32], P('rep', 'cls')
- query_grads: bfloat16 [2, 32, 768], P('rep', 'cls')
- refreshed_vectors: bfloat16 [12288, 768], P(('cls', 'rep'))
Inputs may be any that keep to these rules, and one draw needn't show every extreme that they name: `positives`: each row holds 1 to 4 label ids in its first places and -1 in the rest; ids may repeat within a row. `targets`: A permutation. Refreshed row t belongs to owner t // 768. The b-th aligned block of 384 entries names exactly 24 rows of every owner, all in the half b % 2 of that owner's 768 rows.
All inputs are finite; a program needn't handle non-finite values.
Results may differ from a plain program's by a relative error of at most 0.0048.
Values may be sent and summed in bfloat16 or wider, within the bound.
A program may use at most 128 MiB of HBM per device.

v0:
```python
import functools

import jax
import jax.numpy as jnp
from jax import lax
from jax.experimental import pallas as pl
from jax.experimental.pallas import tpu as pltpu
from jax.sharding import PartitionSpec as P

SLOTS = 8
NEG = -1e30
STATS = 128
NT = (((1,), (1,)), ((), ()))


def to_column(row, eye):
    return jnp.sum(jnp.where(eye, row, 0.0), axis=1, keepdims=True)


def eye_of(n):
    shape = (n, n)
    return lax.broadcasted_iota(jnp.int32, shape, 0) == lax.broadcasted_iota(jnp.int32, shape, 1)


def step_kernel(
    n_cls,
    n_rep,
    slot_ref,
    queries_ref,
    positives_ref,
    targets_ref,
    gain_ref,
    labels_hbm,
    features_hbm,
    weight_hbm,
    free_hbm,
    loss_ref,
    grads_ref,
    refreshed_hbm,
    labels,
    features,
    weight,
    free,
    fresh_rows,
    id_counts,
    q_slots,
    q_rows,
    out_rows,
    in_rows,
    staged,
    logits,
    mixed,
    half_out,
    half_in,
    shares_out,
    shares_in,
    load_sem,
    q_send,
    q_recv,
    relay_send,
    relay_recv,
    fresh_sem,
    row_send,
    row_recv,
    half_send,
    half_recv,
    share_send,
    share_recv,
):
    f32, bf16 = jnp.float32, jnp.bfloat16
    cls = lax.axis_index("cls")
    rep = lax.axis_index("rep")
    total = n_cls * n_rep
    me = cls * n_rep + rep
    half_rows, width = features.shape
    padded = out_rows.shape[1]
    per_owner = half_rows // n_cls
    query_rows = q_slots.shape[1]
    n_query = q_rows.shape[0]
    own_half = n_query // n_rep
    usable, slot_rows = labels.shape[0], half_rows * n_rep
    lab_rows = usable * n_rep

    def slot_of(c, r):
        return r * n_cls + c

    barrier = pltpu.get_barrier_semaphore()

    def greet(k, carry):
        other = lax.rem(me + k, total)
        pl.semaphore_signal(barrier, inc=1, device_id=(other // n_rep, lax.rem(other, n_rep)))
        return carry

    lax.fori_loop(1, total, greet, 0)

    loads = [
        pltpu.make_async_copy(features_hbm, features, load_sem.at[0]),
        pltpu.make_async_copy(weight_hbm, weight, load_sem.at[1]),
        pltpu.make_async_copy(free_hbm, free, load_sem.at[2]),
    ]
    chunks = usable // slot_rows
    for k in range(chunks):
        start = pl.multiple_of(rep * usable + k * slot_rows, slot_rows)
        loads.append(
            pltpu.make_async_copy(
                labels_hbm.at[pl.ds(start, slot_rows)],
                labels.at[pl.ds(k * slot_rows, slot_rows)],
                load_sem.at[3 + k],
            )
        )
    for copy in loads:
        copy.start()

    mine = slot_of(cls, rep)
    q_slots[mine] = queries_ref[0]

    row_i = lax.broadcasted_iota(jnp.int32, (half_rows, half_rows), 0)
    col_i = lax.broadcasted_iota(jnp.int32, (half_rows, half_rows), 1)
    eye = row_i == col_i
    t_row = targets_ref[me].astype(f32)
    t_col = to_column(t_row, eye)
    rank = jnp.sum(jnp.where(t_col < t_row, 1.0, 0.0), axis=0, keepdims=True)
    owner = jnp.floor((rank + 0.5) * (1.0 / per_owner))
    place = owner * padded + (rank - owner * per_owner)
    place_i = lax.broadcasted_iota(jnp.int32, (n_cls * padded, half_rows), 0)
    pick = jnp.where(place_i == place.astype(jnp.int32), 1.0, 0.0).astype(bf16)
    loads[0].wait()
    ordered = jnp.dot(pick, features[...], preferred_element_type=f32).astype(bf16)
    loads[1].wait()
    hidden = jnp.dot(ordered, weight[...], preferred_element_type=f32)
    scale = lax.rsqrt(jnp.mean(hidden * hidden, axis=1, keepdims=True) + 1e-06)
    encoded = hidden * scale * gain_ref[...].reshape(1, width)
    for c in range(n_cls):
        out_rows[c] = encoded[c * padded : (c + 1) * padded].astype(bf16)

    pl.semaphore_wait(barrier, total - 1)

    partner = 1 - rep

    def far(k):
        return lax.rem(cls + 1 + lax.rem(k + n_cls // 2 - 2, n_cls - 1), n_cls)

    def far_from(k):
        return lax.rem(cls + n_cls - 1 - lax.rem(k + n_cls // 2 - 2, n_cls - 1), n_cls)

    def query_copy(other, slot):
        return pltpu.make_async_remote_copy(
            src_ref=q_slots.at[mine],
            dst_ref=q_slots.at[slot],
            send_sem=q_send.at[other],
            recv_sem=q_recv.at[slot],
            device_id=(other, rep),
        )

    def row_copy(other, slot):
        return pltpu.make_async_remote_copy(
            src_ref=out_rows.at[other],
            dst_ref=in_rows.at[slot],
            send_sem=row_send.at[other],
            recv_sem=row_recv.at[slot],
            device_id=(other, rep),
        )

    def share_copy(other, slot):
        return pltpu.make_async_remote_copy(
            src_ref=shares_out.at[other],
            dst_ref=shares_in.at[slot],
            send_sem=share_send.at[other],
            recv_sem=share_recv.at[slot],
            device_id=(other, rep),
        )

    def send_query(k, carry):
        query_copy(far(k), mine).start()
        return carry

    lax.fori_loop(1, n_cls, send_query, 0)

    def send_rows(k, carry):
        row_copy(far(k), cls).start()
        return carry

    lax.fori_loop(1, n_cls, send_rows, 0)
    in_rows[cls] = out_rows[cls]

    def get_query(k, carry):
        other = far_from(k)
        query_copy(other, slot_of(other, rep)).wait_recv()
        return carry

    lax.fori_loop(1, n_cls, get_query, 0)
    side = q_slots.at[pl.ds(rep * n_cls, n_cls)]
    relay = pltpu.make_async_remote_copy(
        src_ref=side,
        dst_ref=side,
        send_sem=relay_send,
        recv_sem=relay_recv,
        device_id=(cls, partner),
    )
    relay.start()

    my_base = (cls * slot_rows + rep * half_rows).astype(f32)
    wanted = my_base + row_i.astype(f32)

    def find(c, acc):
        t_c = targets_ref[c * n_rep + rep].astype(f32)
        return acc + jnp.where(t_c == wanted, (c + 1).astype(f32), 0.0)

    found = lax.fori_loop(0, n_cls, find, jnp.zeros((half_rows, half_rows), f32))
    src_col = jnp.sum(found, axis=1, keepdims=True) - 1.0
    src_row = jnp.sum(jnp.where(eye, src_col, 0.0), axis=0, keepdims=True)
    before = jnp.where((src_col == src_row) & (col_i < row_i), 1.0, 0.0)
    seat = src_col * padded + jnp.sum(before, axis=1, keepdims=True)
    seat_i = lax.broadcasted_iota(jnp.int32, (half_rows, n_cls * padded), 1)
    seating = jnp.where(seat_i == seat.astype(jnp.int32), 1.0, 0.0).astype(bf16)

    relay.wait_recv()
    for s in range(total):
        q_rows[s * query_rows : (s + 1) * query_rows] = q_slots[s].astype(f32)
    q = q_rows[...].astype(bf16)

    n_pos = positives_ref.shape[1]
    eye = eye_of(own_half)
    ids = []
    for p in range(n_pos):
        rows = [positives_ref[r, p : p + 1, :].astype(f32) for r in range(n_rep)]
        ids.append(jnp.concatenate([to_column(row, eye) for row in rows], axis=0).astype(jnp.int32))
    valid = jnp.zeros((n_query, 1), f32)
    for p in range(n_pos):
        valid = valid + jnp.where(ids[p] >= 0, 1.0, 0.0)
    id_counts[...] = jnp.broadcast_to(valid, id_counts.shape)
    slot_start = slot_ref[0] * slot_rows

    def counts_of(first, cols):
        label = first + lax.broadcasted_iota(jnp.int32, (n_query, cols), 1)
        count = jnp.zeros((n_query, cols), f32)
        for p in range(n_pos):
            count = count + jnp.where(ids[p] == label, 1.0, 0.0)
        return count

    def weighted(block, peak, count, vectors):
        power = jnp.exp(block - peak)
        high = power.astype(bf16)
        low = (power - high.astype(f32)).astype(bf16)
        n = n_query
        cols = block.shape[1]
        mixed[0:n, 0:cols] = high
        mixed[n : 2 * n, 0:cols] = low
        mixed[2 * n : 3 * n, 0:cols] = count.astype(bf16)
        out = jnp.dot(mixed[:, 0:cols], vectors, preferred_element_type=f32)
        exp_sum = jnp.sum(power, axis=1, keepdims=True)
        pos_sum = jnp.sum(count * jnp.where(count > 0.0, block, 0.0), axis=1, keepdims=True)
        return out[0:n] + out[n : 2 * n], out[2 * n : 3 * n], exp_sum, pos_sum

    peak = jnp.full((n_query, 1), NEG, f32)
    for k in range(chunks):
        loads[3 + k].wait()
        at = slice(k * slot_rows, (k + 1) * slot_rows)
        block = lax.dot_general(q, labels[at], NT, preferred_element_type=f32)
        fresh = slot_start == rep * usable + k * slot_rows
        block = jnp.where(fresh, NEG, block)
        logits[:, at] = block
        peak = jnp.maximum(peak, jnp.max(block, axis=1, keepdims=True))
    grad = jnp.zeros((n_query, width), f32)
    hits = jnp.zeros((n_query, width), f32)
    exp_sum = jnp.zeros((n_query, 1), f32)
    pos_sum = jnp.zeros((n_query, 1), f32)
    for k in range(chunks):
        at = slice(k * slot_rows, (k + 1) * slot_rows)
        first = cls * lab_rows + rep * usable + k * slot_rows
        fresh = slot_start == rep * usable + k * slot_rows
        count = jnp.where(fresh, 0.0, counts_of(first, slot_rows))
        g, t, e, s = weighted(logits[:, at], peak, count, labels[at])
        grad, hits, exp_sum, pos_sum = grad + g, hits + t, exp_sum + e, pos_sum + s

    fresh_count = counts_of(cls * lab_rows + slot_start + rep * half_rows, half_rows)

    def stage(c):
        staged[pl.ds(pl.multiple_of(c * padded, 8), padded)] = in_rows[c].astype(f32)

    def get_rows(k, carry):
        other = far_from(k)
        row_copy(other, other).wait_recv()
        stage(other)
        return carry

    stage(cls)
    lax.fori_loop(1, n_cls, get_rows, 0)
    placed = jnp.dot(seating, staged[...].astype(bf16), preferred_element_type=f32)
    loads[2].wait()
    fresh_rows[...] = (free[...].astype(f32) + placed).astype(bf16)
    vectors = fresh_rows[...]
    store = pltpu.make_async_copy(fresh_rows, refreshed_hbm, fresh_sem)
    store.start()
    block = lax.dot_general(q, vectors, NT, preferred_element_type=f32)
    fresh_peak = jnp.max(block, axis=1, keepdims=True)
    g, t, e, s = weighted(block, fresh_peak, fresh_count, vectors)
    top = jnp.maximum(peak, fresh_peak)
    a, b = jnp.exp(peak - top), jnp.exp(fresh_peak - top)
    grad, hits = grad * a + g * b, hits + t
    exp_sum, pos_sum = exp_sum * a + e * b, pos_sum + s

    lane = lax.broadcasted_iota(jnp.int32, (n_query, STATS), 1)
    stats = jnp.where(lane == 0, top, jnp.where(lane == 1, exp_sum, pos_sum))
    for r in range(n_rep):
        at = slice(r * own_half, (r + 1) * own_half)
        half_out[r, :, 0:width] = grad[at]
        half_out[r, :, width : 2 * width] = hits[at]
        half_out[r, :, 2 * width :] = stats[at]
    swap = pltpu.make_async_remote_copy(
        src_ref=half_out.at[partner],
        dst_ref=half_in,
        send_sem=half_send,
        recv_sem=half_recv,
        device_id=(cls, partner),
    )
    swap.start()

    def merge(x, y):
        xs, ys = x[:, 2 * width :], y[:, 2 * width :]
        m = jnp.maximum(xs[:, 0:1], ys[:, 0:1])
        a, b = jnp.exp(xs[:, 0:1] - m), jnp.exp(ys[:, 0:1] - m)
        both = x[:, 0:width] * a + y[:, 0:width] * b
        return (
            both,
            x[:, width : 2 * width] + y[:, width : 2 * width],
            m,
            xs[:, 1:2] * a + ys[:, 1:2] * b,
            xs[:, 2:3] + ys[:, 2:3],
        )

    swap.wait_recv()
    both, hits, m, exp_sum, pos_sum = merge(half_out[rep], half_in[...])
    lane = lax.broadcasted_iota(jnp.int32, (own_half, STATS), 1)
    stats = jnp.where(lane == 0, m, jnp.where(lane == 1, exp_sum, pos_sum))
    for c in range(n_cls):
        at = slice(c * query_rows, (c + 1) * query_rows)
        shares_out[c, :, 0:width] = both[at]
        shares_out[c, :, width : 2 * width] = hits[at]
        shares_out[c, :, 2 * width :] = stats[at]

    def send_share(k, carry):
        share_copy(far(k), cls).start()
        return carry

    lax.fori_loop(1, n_cls, send_share, 0)
    shares_in[cls] = shares_out[cls]

    id_count = id_counts[pl.ds(mine * query_rows, query_rows), :][:, 0:1]

    def get_share(k, carry):
        other = far_from(k)
        share_copy(other, other).wait_recv()
        return carry

    lax.fori_loop(1, n_cls, get_share, 0)

    def peak_of(c, m):
        return jnp.maximum(m, shares_in[c, :, 2 * width : 2 * width + 1])

    m = lax.fori_loop(0, n_cls, peak_of, jnp.full((query_rows, 1), NEG, f32))

    def add(c, state):
        grad, hits, exp_sum, pos_sum = state
        share = shares_in[c]
        a = jnp.exp(share[:, 2 * width : 2 * width + 1] - m)
        return (
            grad + a * share[:, 0:width],
            hits + share[:, width : 2 * width],
            exp_sum + a * share[:, 2 * width + 1 : 2 * width + 2],
            pos_sum + share[:, 2 * width + 2 : 2 * width + 3],
        )

    zero = jnp.zeros((query_rows, 1), f32)
    wide = jnp.zeros((query_rows, width), f32)
    grad, hits, exp_sum, pos_sum = lax.fori_loop(0, n_cls, add, (wide, wide, zero, zero))
    loss = m + jnp.log(exp_sum) - pos_sum / id_count
    loss_ref[...] = jnp.sum(jnp.where(eye_of(query_rows), loss, 0.0), axis=0, keepdims=True)
    grads_ref[0] = (grad / exp_sum - hits / id_count).astype(bf16)

    def end_rows(k, carry):
        other = lax.rem(cls + k, n_cls)
        query_copy(other, mine).wait_send()
        row_copy(other, cls).wait_send()
        share_copy(other, cls).wait_send()
        return carry

    lax.fori_loop(1, n_cls, end_rows, 0)
    swap.wait_send()
    relay.wait_send()
    store.wait()


def pass_on(*refs):
    half = len(refs) // 2
    for source, target in zip(refs[:half], refs[half:]):
        target[...] = source[...]


def per_device(
    n_cls,
    n_rep,
    queries,
    positives,
    label_vectors,
    refresh_slot,
    features,
    encoder_weight,
    encoder_gain,
    free_vectors,
    targets,
):
    f32, bf16 = jnp.float32, jnp.bfloat16
    total = n_cls * n_rep
    lab_rows, width = label_vectors.shape
    usable = lab_rows // n_rep
    slot_rows = lab_rows // SLOTS
    half_rows = slot_rows // n_rep
    per_owner = half_rows // n_cls
    padded = -(-per_owner // 8) * 8
    query_rows = queries.shape[1]
    n_query = total * query_rows
    share = 2 * width + STATS
    vmem = pl.BlockSpec(memory_space=pltpu.VMEM)
    smem = pl.BlockSpec(memory_space=pltpu.SMEM)
    hbm = pl.BlockSpec(memory_space=pl.ANY)
    dma = pltpu.SemaphoreType.DMA
    outs = (
        jax.ShapeDtypeStruct((1, query_rows), f32),
        jax.ShapeDtypeStruct((1, query_rows, width), bf16),
        jax.ShapeDtypeStruct((half_rows, width), bf16),
    )
    results = pl.pallas_call(
        functools.partial(step_kernel, n_cls, n_rep),
        out_shape=outs,
        in_specs=[smem, vmem, vmem, vmem, vmem, hbm, hbm, hbm, hbm],
        out_specs=(vmem, vmem, hbm),
        scratch_shapes=[
            pltpu.VMEM((usable, width), bf16),
            pltpu.VMEM((half_rows, width), bf16),
            pltpu.VMEM((width, width), bf16),
            pltpu.VMEM((half_rows, width), bf16),
            pltpu.VMEM((half_rows, width), bf16),
            pltpu.VMEM((n_query, STATS), f32),
            pltpu.VMEM((total, query_rows, width), bf16),
            pltpu.VMEM((n_query, width), f32),
            pltpu.VMEM((n_cls, padded, width), bf16),
            pltpu.VMEM((n_cls, padded, width), bf16),
            pltpu.VMEM((n_cls * padded, width), f32),
            pltpu.VMEM((n_query, usable), f32),
            pltpu.VMEM((3 * n_query, slot_rows), bf16),
            pltpu.VMEM((n_rep, n_query // n_rep, share), f32),
            pltpu.VMEM((n_query // n_rep, share), f32),
            pltpu.VMEM((n_cls, query_rows, share), f32),
            pltpu.VMEM((n_cls, query_rows, share), f32),
            dma((3 + usable // slot_rows,)),
            dma((n_cls,)),
            dma((total,)),
            dma,
            dma,
            dma,
            dma((n_cls,)),
            dma((n_cls,)),
            dma,
            dma,
            dma((n_cls,)),
            dma((n_cls,)),
        ],
        compiler_params=pltpu.CompilerParams(
            collective_id=0, has_side_effects=True, vmem_limit_bytes=60 * 2**20
        ),
    )(
        refresh_slot.reshape(1),
        queries,
        positives.transpose(0, 2, 1),
        targets.reshape(total, 1, half_rows),
        encoder_gain,
        label_vectors,
        features,
        encoder_weight,
        free_vectors,
    )
    return pl.pallas_call(
        pass_on,
        out_shape=outs,
        in_specs=[vmem] * 3,
        out_specs=(vmem,) * 3,
    )(*results)


def solution(mesh):
    placed = (
        P("rep", "cls", None),
        P(),
        P("cls", None),
        P(),
        P(("cls", "rep"), None),
        P(),
        P(),
        P(("cls", "rep"), None),
        P(),
    )
    return jax.shard_map(
        functools.partial(per_device, mesh.shape["cls"], mesh.shape["rep"]),
        mesh=mesh,
        in_specs=placed,
        out_specs=(P("rep", "cls"), P("rep", "cls", None), P(("cls", "rep"), None)),
        check_vma=False,
    )
```

profile of v0, /device:TPU:0, one launch (start us, length us, event | category | flops | bytes accessed | tf_op | source)
XLA Modules:
  0.0 39.2 jit_solution(4133350526121562487)
XLA Ops:
  1.3 36.0 %shard_map.112 = (f32[1,2]{1,0:T(1,128)}, bf16[1,2,768]{2,1,0:T(2,128)(2,1)}, bf16[384,768]{1,0:T(8,128)(2,1)}) custom-call(s32[1]{0:T(128)} %bitcast.3.slot_ref, bf16[1,2,768]{2,1,0:T(2,128)(2,1)} %queries_ref.1, s32[2,4,32]{2,1,0:T(4,128)} %bitcast.5, s32[32,1,384]{2,1,0:T(1,128)} %bitcast.4, f32[768]{0:T(1024)} %gain_ref.1, bf16[6144,768]{1,0:T(8,128)(2,1)} %labels_hbm.1, ...), custom_call_target="tpu_custom_call" | custom-call | tf_op jit(solution)/shard_map/pallas_call | solution.py:433
  37.3 1.9 %shard_map.113 = (f32[1,2]{1,0:T(1,128)}, bf16[1,2,768]{2,1,0:T(2,128)(2,1)}, bf16[384,768]{1,0:T(8,128)(2,1)}) custom-call(f32[1,2]{1,0:T(1,128)} %get-tuple-element.6.refs_0_, bf16[1,2,768]{2,1,0:T(2,128)(2,1)} %get-tuple-element.7.refs_1_, bf16[384,768]{1,0:T(8,128)(2,1)} %get-tuple-element.8.refs_2_), custom_call_target="tpu_custom_call" | custom-call | tf_op jit(solution)/shard_map/pallas_call | solution.py:483
where the time goes:
time: 39.4 us; the launch traced here: 39.2 us
  Pallas kernels  38 us (96%)
  between operations  1.29 us (3%)
    pallas_call x1, Pallas kernels, per_device(): pl.pallas_call(functools.partial(step_kernel, n_cls, n_rep), out_shape=ou...  36 us
    pallas_call x1, Pallas kernels, per_device(): pl.pallas_call(pass_on, out_shape=outs, in_specs=[vmem] * 3, out_specs=(v...  1.93 us

commit v1 on v0

v1 whole, which is shorter than its diff:
```python
import functools

import jax
import jax.numpy as jnp
from jax import lax
from jax.experimental import pallas as pl
from jax.experimental.pallas import tpu as pltpu
from jax.sharding import PartitionSpec as P

SLOTS = 8
NEG = -1e30
STATS = 128
PARTS = 4
NT = (((1,), (1,)), ((), ()))


def to_column(row, eye):
    return jnp.sum(jnp.where(eye, row, 0.0), axis=1, keepdims=True)


def to_row(col, eye):
    return jnp.sum(jnp.where(eye, col, 0.0), axis=0, keepdims=True)


def eye_of(n):
    shape = (n, n)
    return lax.broadcasted_iota(jnp.int32, shape, 0) == lax.broadcasted_iota(jnp.int32, shape, 1)


def each(count, step):
    if count <= 16:
        for i in range(count):
            step(i)
    else:
        lax.fori_loop(0, count, lambda i, carry: (step(i), carry)[1], 0)


def thirds(x):
    f32, bf16 = jnp.float32, jnp.bfloat16
    high = x.astype(bf16).astype(f32)
    rest = x - high
    mid = rest.astype(bf16).astype(f32)
    return high, mid, rest - mid


def step_kernel(
    n_cls,
    n_rep,
    slot_hbm,
    queries_hbm,
    positives_hbm,
    targets_hbm,
    gain_hbm,
    labels_hbm,
    features_hbm,
    weight_hbm,
    free_hbm,
    loss_ref,
    grads_ref,
    refreshed_ref,
    slot_ref,
    positives_ref,
    targets_ref,
    gain_ref,
    labels,
    features,
    weight,
    free,
    free_seats,
    seating,
    fresh_rows,
    id_counts,
    q_slots,
    q_rows,
    out_rows,
    in_rows,
    logits,
    mixed,
    half_out,
    half_in,
    hits_out,
    hits_in,
    shares_out,
    shares_in,
    load_sem,
    q_sem,
    relay_sem,
    row_send,
    row_recv,
    half_sem,
    share_sem,
):
    f32, bf16 = jnp.float32, jnp.bfloat16
    cls = lax.axis_index("cls")
    rep = lax.axis_index("rep")
    partner = 1 - rep
    me = cls * n_rep + rep
    half_rows, width = features.shape
    padded = out_rows.shape[1]
    per_owner = half_rows // n_cls
    query_rows = q_slots.shape[1]
    n_query = q_rows.shape[0]
    own_half = n_query // n_rep
    usable, slot_rows = labels.shape[0], half_rows * n_rep
    lab_rows = usable * n_rep
    seats = n_cls * padded
    mine = rep * n_cls + cls

    barrier = pltpu.get_barrier_semaphore()

    def greet(i):
        pl.semaphore_signal(barrier, inc=1, device_id=(cls ^ (n_cls - 1 - i), rep))

    each(n_cls - 1, greet)
    pl.semaphore_signal(barrier, inc=1, device_id=(cls, partner))

    chunks = usable // slot_rows
    pairs = [
        (features_hbm, features),
        (targets_hbm, targets_ref),
        (weight_hbm, weight),
        (gain_hbm, gain_ref),
        (queries_hbm.at[0], q_slots.at[mine]),
        (slot_hbm, slot_ref),
        (positives_hbm, positives_ref),
        (free_hbm, free),
    ]
    for k in range(chunks):
        start = pl.multiple_of(rep * usable + k * slot_rows, slot_rows)
        pairs.append((labels_hbm.at[pl.ds(start, slot_rows)], labels.at[pl.ds(k * slot_rows, slot_rows)]))
    loads = [pltpu.make_async_copy(a, b, load_sem.at[i]) for i, (a, b) in enumerate(pairs)]
    for copy in loads:
        copy.start()

    row_i = lax.broadcasted_iota(jnp.int32, (half_rows, half_rows), 0)
    col_i = lax.broadcasted_iota(jnp.int32, (half_rows, half_rows), 1)
    eye = row_i == col_i
    loads[1].wait()
    t_row = targets_ref[me].astype(f32)
    t_col = to_column(t_row, eye)
    rank = jnp.sum(jnp.where(t_col < t_row, 1.0, 0.0), axis=0, keepdims=True)
    owner = jnp.floor((rank + 0.5) * (1.0 / per_owner))
    seat_in = (rank - owner * per_owner).astype(jnp.int32)
    place = (owner.astype(jnp.int32) ^ cls) * padded + seat_in
    place_i = lax.broadcasted_iota(jnp.int32, (seats, half_rows), 0)
    pick = jnp.where(place_i == place, 1.0, 0.0).astype(bf16)
    loads[0].wait()
    ordered = jnp.dot(pick, features[...], preferred_element_type=f32).astype(bf16)
    loads[2].wait()
    hidden = jnp.dot(ordered, weight[...], preferred_element_type=f32)
    scale = lax.rsqrt(jnp.mean(hidden * hidden, axis=1, keepdims=True) + 1e-06)
    loads[3].wait()
    encoded = hidden * scale * gain_ref[...].reshape(1, width)
    for k in range(n_cls):
        out_rows[k] = encoded[k * padded : (k + 1) * padded].astype(bf16)
    loads[4].wait()

    pl.semaphore_wait(barrier, n_cls)

    def query_copy(k, slot, many):
        return pltpu.make_async_remote_copy(
            src_ref=q_slots.at[pl.ds(slot, many)],
            dst_ref=q_slots.at[pl.ds(slot, many)],
            send_sem=q_sem.at[0],
            recv_sem=q_sem.at[1],
            device_id=(cls ^ k, rep),
        )

    def row_copy(k, slot, many, part):
        return pltpu.make_async_remote_copy(
            src_ref=out_rows.at[pl.ds(slot, many)],
            dst_ref=in_rows.at[pl.ds(slot, many)],
            send_sem=row_send,
            recv_sem=row_recv.at[part],
            device_id=(cls ^ k, rep),
        )

    def share_copy(k, source, slot, many):
        return pltpu.make_async_remote_copy(
            src_ref=shares_out.at[pl.ds(source, many)],
            dst_ref=shares_in.at[pl.ds(slot, many)],
            send_sem=share_sem.at[0],
            recv_sem=share_sem.at[1],
            device_id=(cls ^ k, rep),
        )

    each(n_cls - 1, lambda i: query_copy(n_cls - 1 - i, mine, 1).start())
    span = n_cls // PARTS
    for part in reversed(range(PARTS)):
        top = (part + 1) * span - 1
        count = span if part else span - 1
        each(count, lambda i, top=top, part=part: row_copy(top - i, top - i, 1, part).start())
    in_rows[0] = out_rows[0]

    my_base = cls * slot_rows + rep * half_rows
    wanted = my_base.astype(f32) + row_i.astype(f32)

    def find(c, acc):
        t_c = targets_ref[c * n_rep + rep].astype(f32)
        return acc + jnp.where(t_c == wanted, (c + 1).astype(f32), 0.0)

    found = lax.fori_loop(0, n_cls, find, jnp.zeros((half_rows, half_rows), f32))
    src_col = jnp.sum(found, axis=1, keepdims=True) - 1.0
    src_row = to_row(src_col, eye)
    before = jnp.where((src_col == src_row) & (col_i < row_i), 1.0, 0.0)
    count_col = jnp.sum(before, axis=1, keepdims=True)
    seat_col = (src_col.astype(jnp.int32) ^ cls) * padded + count_col.astype(jnp.int32)
    seat_row = to_row(seat_col.astype(f32), eye).astype(jnp.int32)
    seat_i = lax.broadcasted_iota(jnp.int32, (half_rows, seats), 1)
    seating[...] = jnp.where(seat_i == seat_col, 1.0, 0.0).astype(bf16)
    turned_i = lax.broadcasted_iota(jnp.int32, (seats, half_rows), 0)
    turned = jnp.where(turned_i == seat_row, 1.0, 0.0).astype(bf16)
    loads[7].wait()
    free_seats[...] = jnp.dot(turned, free[...], preferred_element_type=f32)

    loads[5].wait()
    loads[6].wait()
    n_pos = positives_ref.shape[1]
    eye = eye_of(own_half)
    ids = []
    for p in range(n_pos):
        rows = [positives_ref[r, p : p + 1, :].astype(f32) for r in range(n_rep)]
        ids.append(jnp.concatenate([to_column(row, eye) for row in rows], axis=0).astype(jnp.int32))
    valid = jnp.zeros((n_query, 1), f32)
    for p in range(n_pos):
        valid = valid + jnp.where(ids[p] >= 0, 1.0, 0.0)
    id_counts[...] = jnp.broadcast_to(valid, id_counts.shape)
    slot_start = slot_ref[0] * slot_rows

    def counts_of(label):
        count = jnp.zeros((n_query, label.shape[1]), f32)
        for p in range(n_pos):
            count = count + jnp.where(ids[p] == label, 1.0, 0.0)
        return count

    part_rows = span * padded
    fresh_base = cls * lab_rows + slot_start + rep * half_rows
    fresh_seen, fresh_count = [], []
    for part in range(PARTS):
        at_i = part * part_rows + lax.broadcasted_iota(jnp.int32, (half_rows, part_rows), 1)
        row_f = lax.broadcasted_iota(jnp.int32, (half_rows, part_rows), 0).astype(f32)
        at_row = jnp.sum(jnp.where(at_i == seat_col, row_f + 1.0, 0.0), axis=0, keepdims=True)
        at_row = at_row.astype(jnp.int32)
        fresh_seen.append(at_row > 0)
        fresh_count.append(counts_of(jnp.where(at_row > 0, fresh_base - 1 + at_row, -2)))

    query_copy(1, 0, n_cls - 1).wait_recv()
    side = q_slots.at[pl.ds(rep * n_cls, n_cls)]
    relay = pltpu.make_async_remote_copy(
        src_ref=side,
        dst_ref=side,
        send_sem=relay_sem.at[0],
        recv_sem=relay_sem.at[1],
        device_id=(cls, partner),
    )
    relay.start()
    relay.wait_recv()
    for s in range(n_cls * n_rep):
        q_rows[s * query_rows : (s + 1) * query_rows] = q_slots[s].astype(f32)
    q = q_rows[...].astype(bf16)

    def split(power):
        high = power.astype(bf16)
        return high, (power - high.astype(f32)).astype(bf16)

    def sums(block, power, count):
        exp_sum = jnp.sum(power, axis=1, keepdims=True)
        pos_sum = jnp.sum(count * jnp.where(count > 0.0, block, 0.0), axis=1, keepdims=True)
        return exp_sum, pos_sum

    n = n_query
    peak = jnp.full((n, 1), NEG, f32)
    for k in range(chunks):
        loads[8 + k].wait()
        at = slice(k * slot_rows, (k + 1) * slot_rows)
        block = lax.dot_general(q, labels[at], NT, preferred_element_type=f32)
        fresh = slot_start == rep * usable + k * slot_rows
        block = jnp.where(fresh, NEG, block)
        logits[:, at] = block
        peak = jnp.maximum(peak, jnp.max(block, axis=1, keepdims=True))
    grad = jnp.zeros((n, width), f32)
    hits = jnp.zeros((n, width), f32)
    exp_sum = jnp.zeros((n, 1), f32)
    pos_sum = jnp.zeros((n, 1), f32)
    for k in range(chunks):
        at = slice(k * slot_rows, (k + 1) * slot_rows)
        first = cls * lab_rows + rep * usable + k * slot_rows
        fresh = slot_start == rep * usable + k * slot_rows
        label = first + lax.broadcasted_iota(jnp.int32, (n, slot_rows), 1)
        count = jnp.where(fresh, 0.0, counts_of(label))
        block = logits[:, at]
        power = jnp.exp(block - peak)
        mixed[0:n], mixed[n : 2 * n] = split(power)
        mixed[2 * n : 3 * n] = count.astype(bf16)
        out = jnp.dot(mixed[...], labels[at], preferred_element_type=f32)
        e, s = sums(block, power, count)
        grad = grad + (out[0:n] + out[n : 2 * n])
        hits, exp_sum, pos_sum = hits + out[2 * n : 3 * n], exp_sum + e, pos_sum + s

    for part in [PARTS - 1, *range(PARTS - 1)]:
        low = part * span if part else 1
        row_copy(1, low, (part + 1) * span - low, part).wait_recv()
        at = slice(part * part_rows, (part + 1) * part_rows)
        landed = [in_rows[k].astype(f32) for k in range(part * span, (part + 1) * span)]
        vectors = (free_seats[at] + jnp.concatenate(landed, axis=0)).astype(bf16)
        fresh_rows[at] = vectors
        block = lax.dot_general(q, vectors, NT, preferred_element_type=f32)
        block = jnp.where(fresh_seen[part], block, NEG)
        top = jnp.maximum(peak, jnp.max(block, axis=1, keepdims=True))
        power = jnp.exp(block - top)
        high, rest = split(power)
        count = fresh_count[part]
        out = jnp.dot(
            jnp.concatenate([high, rest, count.astype(bf16)], axis=0), vectors, preferred_element_type=f32
        )
        e, s = sums(block, power, count)
        a = jnp.exp(peak - top)
        grad = grad * a + (out[0:n] + out[n : 2 * n])
        hits, exp_sum, pos_sum = hits + out[2 * n : 3 * n], exp_sum * a + e, pos_sum + s
        peak = top

    lane = lax.broadcasted_iota(jnp.int32, (n, STATS), 1)
    stats = jnp.where(lane == 0, peak, jnp.where(lane == 1, exp_sum, pos_sum))
    for r in range(n_rep):
        at = slice(r * own_half, (r + 1) * own_half)
        half_out[r, :, 0:width] = grad[at]
        half_out[r, :, width:] = stats[at]
        hits_out[r] = hits[at].astype(bf16)
    swaps = []
    for i, (a, b) in enumerate([(half_out, half_in), (hits_out, hits_in)]):
        swap = pltpu.make_async_remote_copy(
            src_ref=a.at[partner],
            dst_ref=b,
            send_sem=half_sem.at[i],
            recv_sem=half_sem.at[2 + i],
            device_id=(cls, partner),
        )
        swap.start()
        swaps.append(swap)
    x, xh = half_out[rep], hits_out[rep].astype(f32)
    some = id_counts[pl.ds(pl.multiple_of(rep * own_half, own_half), own_half), :][:, 0:1]
    for swap in swaps:
        swap.wait_recv()
    y, yh = half_in[...], hits_in[...].astype(f32)
    xs, ys = x[:, width:], y[:, width:]
    m = jnp.maximum(xs[:, 0:1], ys[:, 0:1])
    a, b = jnp.exp(xs[:, 0:1] - m), jnp.exp(ys[:, 0:1] - m)
    exp_sum = xs[:, 1:2] * a + ys[:, 1:2] * b
    pos_sum = xs[:, 2:3] + ys[:, 2:3]
    hits = xh + yh
    inv = 1.0 / exp_sum
    term = x[:, 0:width] * (a * inv) + y[:, 0:width] * (b * inv) - hits * (1.0 / some)
    lane = lax.broadcasted_iota(jnp.int32, (own_half, STATS), 1)
    stats = jnp.zeros((own_half, STATS), f32)
    for i, value in enumerate([m, exp_sum, pos_sum]):
        for j, piece in enumerate(thirds(value)):
            stats = jnp.where(lane == 3 * j + i, piece, stats)
    term, hits, stats = term.astype(bf16), hits.astype(bf16), stats.astype(bf16)
    for c in range(n_cls):
        at = slice(c * query_rows, (c + 1) * query_rows)
        shares_out[c, :, 0:width] = term[at]
        shares_out[c, :, width : 2 * width] = hits[at]
        shares_out[c, :, 2 * width :] = stats[at]

    def send_share(i):
        k = n_cls - 1 - i
        share_copy(k, cls ^ k, k, 1).start()

    each(n_cls - 1, send_share)
    shares_in[0] = shares_out[cls]

    refreshed = jnp.dot(seating[...], fresh_rows[...], preferred_element_type=f32)
    refreshed_ref[...] = refreshed.astype(bf16)
    query_copy(1, 0, n_cls - 1).wait_send()
    row_copy(1, 1, n_cls - 1, 0).wait_send()
    relay.wait_send()
    for swap in swaps:
        swap.wait_send()
    id_count = id_counts[pl.ds(mine * query_rows, query_rows), :][:, 0:1]

    share_copy(1, 0, 1, n_cls - 1).wait_recv()
    stats = shares_in[:, :, 2 * width :].astype(f32)
    stats = stats[:, :, 0:3] + stats[:, :, 3:6] + stats[:, :, 6:9]
    ms, es = stats[:, :, 0:1], stats[:, :, 1:2]
    pos_sum = jnp.sum(stats[:, :, 2:3], axis=0)
    m = jnp.max(ms, axis=0)
    es = es * jnp.exp(ms - m[None])
    exp_sum = jnp.sum(es, axis=0)
    rho = es * (1.0 / exp_sum)[None]
    inv = 1.0 / id_count
    back = (rho - 1.0) * inv[None]
    grad = jnp.zeros((query_rows, width), f32)
    for k in range(n_cls):
        grad = grad + rho[k] * shares_in[k, :, 0:width].astype(f32)
        grad = grad + back[k] * shares_in[k, :, width : 2 * width].astype(f32)
    loss = m + jnp.log(exp_sum) - pos_sum / id_count
    loss_ref[...] = to_row(loss, eye_of(query_rows))
    grads_ref[0] = grad.astype(bf16)
    share_copy(1, 0, 1, n_cls - 1).wait_send()


def pass_on(*refs):
    sem = refs[-1]
    half = len(refs) // 2
    copies = []
    for i, (source, target) in enumerate(zip(refs[:half], refs[half:-1])):
        copy = pltpu.make_async_copy(source, target, sem.at[i])
        copy.start()
        copies.append(copy)
    for copy in copies:
        copy.wait()


def per_device(
    n_cls,
    n_rep,
    queries,
    positives,
    label_vectors,
    refresh_slot,
    features,
    encoder_weight,
    encoder_gain,
    free_vectors,
    targets,
):
    f32, bf16 = jnp.float32, jnp.bfloat16
    total = n_cls * n_rep
    lab_rows, width = label_vectors.shape
    usable = lab_rows // n_rep
    slot_rows = lab_rows // SLOTS
    half_rows = slot_rows // n_rep
    per_owner = half_rows // n_cls
    padded = -(-per_owner // 8) * 8
    query_rows = queries.shape[1]
    n_query = total * query_rows
    own_half = n_query // n_rep
    n_pos = positives.shape[2]
    share = 2 * width + STATS
    vmem = pl.BlockSpec(memory_space=pltpu.VMEM)
    hbm = pl.BlockSpec(memory_space=pl.ANY)
    dma = pltpu.SemaphoreType.DMA
    outs = (
        ((1, query_rows), f32),
        ((1, query_rows, width), bf16),
        ((half_rows, width), bf16),
    )
    results = pl.pallas_call(
        functools.partial(step_kernel, n_cls, n_rep),
        out_shape=tuple(pltpu.VMEM(*out) for out in outs),
        in_specs=[hbm] * 9,
        out_specs=(vmem,) * 3,
        scratch_shapes=[
            pltpu.SMEM((1,), jnp.int32),
            pltpu.VMEM((n_rep, n_pos, own_half), jnp.int32),
            pltpu.VMEM((total, 1, half_rows), jnp.int32),
            pltpu.VMEM((width,), f32),
            pltpu.VMEM((usable, width), bf16),
            pltpu.VMEM((half_rows, width), bf16),
            pltpu.VMEM((width, width), bf16),
            pltpu.VMEM((half_rows, width), bf16),
            pltpu.VMEM((n_cls * padded, width), f32),
            pltpu.VMEM((half_rows, n_cls * padded), bf16),
            pltpu.VMEM((n_cls * padded, width), bf16),
            pltpu.VMEM((n_query, STATS), f32),
            pltpu.VMEM((total, query_rows, width), bf16),
            pltpu.VMEM((n_query, width), f32),
            pltpu.VMEM((n_cls, padded, width), bf16),
            pltpu.VMEM((n_cls, padded, width), bf16),
            pltpu.VMEM((n_query, usable), f32),
            pltpu.VMEM((3 * n_query, slot_rows), bf16),
            pltpu.VMEM((n_rep, own_half, width + STATS), f32),
            pltpu.VMEM((own_half, width + STATS), f32),
            pltpu.VMEM((n_rep, own_half, width), bf16),
            pltpu.VMEM((own_half, width), bf16),
            pltpu.VMEM((n_cls, query_rows, share), bf16),
            pltpu.VMEM((n_cls, query_rows, share), bf16),
            dma((8 + usable // slot_rows,)),
            dma((2,)),
            dma((2,)),
            dma,
            dma((PARTS,)),
            dma((4,)),
            dma((2,)),
        ],
        compiler_params=pltpu.CompilerParams(
            collective_id=0, has_side_effects=True, vmem_limit_bytes=48 * 2**20
        ),
    )(
        refresh_slot.reshape(1),
        queries,
        positives.transpose(0, 2, 1),
        targets.reshape(total, 1, half_rows),
        encoder_gain,
        label_vectors,
        features,
        encoder_weight,
        free_vectors,
    )
    return pl.pallas_call(
        pass_on,
        out_shape=tuple(jax.ShapeDtypeStruct(*out) for out in outs),
        in_specs=[vmem] * 3,
        out_specs=(hbm,) * 3,
        scratch_shapes=[dma((3,))],
    )(*results)


def solution(mesh):
    placed = (
        P("rep", "cls", None),
        P(),
        P("cls", None),
        P(),
        P(("cls", "rep"), None),
        P(),
        P(),
        P(("cls", "rep"), None),
        P(),
    )
    return jax.shard_map(
        functools.partial(per_device, mesh.shape["cls"], mesh.shape["rep"]),
        mesh=mesh,
        in_specs=placed,
        out_specs=(P("rep", "cls"), P("rep", "cls", None), P(("cls", "rep"), None)),
        check_vma=False,
    )
```

time: 39.4 us -> 42 us (1.066)
  local copies, waits for them, and re-layouts: 0 us -> 8.21 us
  Pallas kernels: 38 us -> 32 us
    unnamed x0 -> x20, local copies, waits for them, and re-layouts: none -> 8.21 us
    pallas_call x2, Pallas kernels: 38 us -> 32 us  [the longest x1 30.1 us: per_device(): pl.pallas_call(functools.partial(step_kernel, n_cls, n_rep), out_shape=tu...]
where the time goes in v1:
time: 42 us; the launch traced here: 41.6 us
  Pallas kernels  32 us (76%)
  local copies, waits for them, and re-layouts  8.21 us (20%)
  between operations  1.31 us (3%)
    pallas_call x1, Pallas kernels, per_device(): pl.pallas_call(functools.partial(step_kernel, n_cls, n_rep), out_shape=tu...  30.1 us
    unnamed x20, local copies, waits for them, and re-layouts  8.21 us
    pallas_call x1, Pallas kernels, per_device(): pl.pallas_call(pass_on, out_shape=tuple((jax.ShapeDtypeStruct(*out) for o...  1.92 us

profile of v1, /device:TPU:0, one launch (start us, length us, event | category | flops | bytes accessed | tf_op | source)
XLA Modules:
  0.0 41.6 jit_solution(10956561916476279450)
XLA Ops:
  1.3 0.0 copy-start
  1.3 1.3 %copy-done = bf16[768,768]{1,0:T(8,128)(2,1)S(1)} copy-done((bf16[768,768]{1,0:T(8,128)(2,1)S(1)}, bf16[768,768]{1,0:T(8,128)(2,1)}, u32[]{:S(2)}) %copy-start) | copy-done | bytes 1179672
  2.6 0.0 copy-start.1
  2.6 1.1 %copy-done.1 = bf16[384,768]{1,0:T(8,128)(2,1)S(1)} copy-done((bf16[384,768]{1,0:T(8,128)(2,1)S(1)}, bf16[384,768]{1,0:T(8,128)(2,1)}, u32[]{:S(2)}) %copy-start.1) | copy-done | bytes 589848
  3.6 0.0 copy-start.2
  3.6 1.1 %copy-done.2 = bf16[384,768]{1,0:T(8,128)(2,1)S(1)} copy-done((bf16[384,768]{1,0:T(8,128)(2,1)S(1)}, bf16[384,768]{1,0:T(8,128)(2,1)}, u32[]{:S(2)}) %copy-start.2) | copy-done | bytes 589848
  4.7 0.0 copy-start.4
  4.7 0.8 %copy-done.4 = s32[12288]{0:T(1024)S(1)} copy-done((s32[12288]{0:T(1024)S(1)}, s32[12288]{0:T(1024)}, u32[]{:S(2)}) %copy-start.4) | copy-done | bytes 49176
  5.5 0.0 copy-start.5
  5.5 0.7 %copy-done.5 = s32[2,32,4]{1,2,0:T(4,128)S(1)} copy-done((s32[2,32,4]{1,2,0:T(4,128)S(1)}, s32[2,32,4]{1,2,0:T(4,128)}, u32[]{:S(2)}) %copy-start.5) | copy-done | bytes 1048
  6.2 0.0 copy-start.6
  6.2 0.7 %copy-done.6 = f32[768]{0:T(1024)S(1)} copy-done((f32[768]{0:T(1024)S(1)}, f32[768]{0:T(1024)}, u32[]{:S(2)}) %copy-start.6) | copy-done | bytes 3096
  6.9 0.0 copy-start.7
  6.9 0.7 %copy-done.7 = bf16[1,2,768]{2,1,0:T(2,128)(2,1)S(1)} copy-done((bf16[1,2,768]{2,1,0:T(2,128)(2,1)S(1)}, bf16[1,2,768]{2,1,0:T(2,128)(2,1)}, u32[]{:S(2)}) %copy-start.7) | copy-done | bytes 3096
  7.5 30.1 %shard_map.112 = (f32[1,2]{1,0:T(1,128)S(1)}, bf16[1,2,768]{2,1,0:T(2,128)(2,1)S(1)}, bf16[384,768]{1,0:T(8,128)(2,1)S(1)}) custom-call(s32[1]{0:T(128)} %bitcast.3.slot_hbm, bf16[1,2,768]{2,1,0:T(2,128)(2,1)S(1)} %copy-done.7, s32[2,4,32]{2,1,0:T(4,128)S(1)} %bitcast.5, s32[32,1,384]{2,1,0:T(1,128)S(1)} %bitcast.4, f32[768]{0:T(1024)S(1)} %copy-done.6, ...), custom_call_target="tpu_custom_call" | custom-call | tf_op jit(solution)/shard_map/pallas_call | solution.py:448
  37.7 0.0 copy-start.3
  37.7 0.8 %copy-done.3 = bf16[384,768]{1,0:T(8,128)(2,1)} copy-done((bf16[384,768]{1,0:T(8,128)(2,1)}, bf16[384,768]{1,0:T(8,128)(2,1)S(1)}, u32[]{:S(2)}) %copy-start.3) | copy-done | bytes 589848
  38.5 0.0 copy-start.8
  38.5 0.6 %copy-done.8 = bf16[1,2,768]{2,1,0:T(2,128)(2,1)} copy-done((bf16[1,2,768]{2,1,0:T(2,128)(2,1)}, bf16[1,2,768]{2,1,0:T(2,128)(2,1)S(1)}, u32[]{:S(2)}) %copy-start.8) | copy-done | bytes 3096
  39.1 0.0 copy-start.9
  39.1 0.6 %copy-done.9 = f32[1,2]{1,0:T(1,128)} copy-done((f32[1,2]{1,0:T(1,128)}, f32[1,2]{1,0:T(1,128)S(1)}, u32[]{:S(2)}) %copy-start.9) | copy-done | bytes 32
  39.6 1.9 %shard_map.113 = (f32[1,2]{1,0:T(1,128)}, bf16[1,2,768]{2,1,0:T(2,128)(2,1)}, bf16[384,768]{1,0:T(8,128)(2,1)}) custom-call(f32[1,2]{1,0:T(1,128)} %copy-done.9, bf16[1,2,768]{2,1,0:T(2,128)(2,1)} %copy-done.8, bf16[384,768]{1,0:T(8,128)(2,1)} %copy-done.3), custom_call_target="tpu_custom_call" | custom-call | tf_op jit(solution)/shard_map/pallas_call | solution.py:500
Async XLA Ops:
  1.3 1.3 %copy-start = (bf16[768,768]{1,0:T(8,128)(2,1)S(1)}, bf16[768,768]{1,0:T(8,128)(2,1)}, u32[]{:S(2)}) copy-start(bf16[768,768]{1,0:T(8,128)(2,1)} %weight_hbm.1) | copy-start | bytes 3538948
  2.6 1.1 %copy-start.1 = (bf16[384,768]{1,0:T(8,128)(2,1)S(1)}, bf16[384,768]{1,0:T(8,128)(2,1)}, u32[]{:S(2)}) copy-start(bf16[384,768]{1,0:T(8,128)(2,1)} %features_hbm.1) | copy-start | bytes 1769476
  3.6 1.1 %copy-start.2 = (bf16[384,768]{1,0:T(8,128)(2,1)S(1)}, bf16[384,768]{1,0:T(8,128)(2,1)}, u32[]{:S(2)}) copy-start(bf16[384,768]{1,0:T(8,128)(2,1)} %free_hbm.1) | copy-start | bytes 1769476
  4.7 0.8 %copy-start.4 = (s32[12288]{0:T(1024)S(1)}, s32[12288]{0:T(1024)}, u32[]{:S(2)}) copy-start(s32[12288]{0:T(1024)} %param.17) | copy-start | bytes 147460
  5.5 0.7 %copy-start.5 = (s32[2,32,4]{1,2,0:T(4,128)S(1)}, s32[2,32,4]{1,2,0:T(4,128)}, u32[]{:S(2)}) copy-start(s32[2,32,4]{1,2,0:T(4,128)} %param.10) | copy-start | bytes 3076
  6.2 0.7 %copy-start.6 = (f32[768]{0:T(1024)S(1)}, f32[768]{0:T(1024)}, u32[]{:S(2)}) copy-start(f32[768]{0:T(1024)} %gain_hbm.1) | copy-start | bytes 9220
  6.9 0.7 %copy-start.7 = (bf16[1,2,768]{2,1,0:T(2,128)(2,1)S(1)}, bf16[1,2,768]{2,1,0:T(2,128)(2,1)}, u32[]{:S(2)}) copy-start(bf16[1,2,768]{2,1,0:T(2,128)(2,1)} %queries_hbm.1) | copy-start | bytes 9220
  37.7 0.8 %copy-start.3 = (bf16[384,768]{1,0:T(8,128)(2,1)}, bf16[384,768]{1,0:T(8,128)(2,1)S(1)}, u32[]{:S(2)}) copy-start(bf16[384,768]{1,0:T(8,128)(2,1)S(1)} %get-tuple-element.8.refs_2_) | copy-start | bytes 1769476
  38.5 0.6 %copy-start.8 = (bf16[1,2,768]{2,1,0:T(2,128)(2,1)}, bf16[1,2,768]{2,1,0:T(2,128)(2,1)S(1)}, u32[]{:S(2)}) copy-start(bf16[1,2,768]{2,1,0:T(2,128)(2,1)S(1)} %get-tuple-element.7.refs_1_) | copy-start | bytes 9220
  39.1 0.6 %copy-start.9 = (f32[1,2]{1,0:T(1,128)}, f32[1,2]{1,0:T(1,128)S(1)}, u32[]{:S(2)}) copy-start(f32[1,2]{1,0:T(1,128)S(1)} %get-tuple-element.6.refs_0_) | copy-start | bytes 28

commit v2 on v1

--- a/solution.py
+++ b/solution.py
@@ -185,6 +185,7 @@
         )
 
     each(n_cls - 1, lambda i: query_copy(n_cls - 1 - i, mine, 1).start())
+    query_copy(1, 0, n_cls - 1).wait_send()
     span = n_cls // PARTS
     for part in reversed(range(PARTS)):
         top = (part + 1) * span - 1
@@ -371,7 +372,6 @@
 
     refreshed = jnp.dot(seating[...], fresh_rows[...], preferred_element_type=f32)
     refreshed_ref[...] = refreshed.astype(bf16)
-    query_copy(1, 0, n_cls - 1).wait_send()
     row_copy(1, 1, n_cls - 1, 0).wait_send()
     relay.wait_send()
     for swap in swaps:
@@ -438,7 +438,7 @@
     n_pos = positives.shape[2]
     share = 2 * width + STATS
     vmem = pl.BlockSpec(memory_space=pltpu.VMEM)
-    hbm = pl.BlockSpec(memory_space=pl.ANY)
+    hbm = pl.BlockSpec(memory_space=pltpu.HBM)
     dma = pltpu.SemaphoreType.DMA
     outs = (
         ((1, query_rows), f32),
@@ -488,14 +488,19 @@
         ),
     )(
         refresh_slot.reshape(1),
-        queries,
-        positives.transpose(0, 2, 1),
-        targets.reshape(total, 1, half_rows),
-        encoder_gain,
-        label_vectors,
-        features,
-        encoder_weight,
-        free_vectors,
+        *[
+            pltpu.with_memory_space_constraint(x, pltpu.HBM)
+            for x in (
+                queries,
+                positives.transpose(0, 2, 1),
+                targets.reshape(total, 1, half_rows),
+                encoder_gain,
+                label_vectors,
+                features,
+                encoder_weight,
+                free_vectors,
+            )
+        ]
     )
     return pl.pallas_call(
         pass_on,
@@ -503,7 +508,7 @@
         in_specs=[vmem] * 3,
         out_specs=(hbm,) * 3,
         scratch_shapes=[dma((3,))],
-    )(*results)
+    )(*[pltpu.with_memory_space_constraint(x, pltpu.VMEM) for x in results])
 
 
 def solution(mesh):

time: 42 us -> 30.7 us (0.73)
  local copies, waits for them, and re-layouts: 8.21 us -> 0 us
  Pallas kernels: 32 us -> 29.1 us
    unnamed x20 -> x0, local copies, waits for them, and re-layouts: 8.21 us -> none
    pallas_call x1, Pallas kernels: 30.1 us -> 28.2 us  [per_device(): pl.pallas_call(functools.partial(step_kernel, n_cls, n_rep), out_shape=tu...]
    pallas_call x1, Pallas kernels: 1.92 us -> 0.85 us  [per_device(): pl.pallas_call(pass_on, out_shape=tuple((jax.ShapeDtypeStruct(*out) for o...]
where the time goes in v2:
time: 30.7 us; the launch traced here: 30.4 us
  Pallas kernels  29.1 us (95%)
  between operations  1.29 us (4%)
    pallas_call x1, Pallas kernels, per_device(): pl.pallas_call(functools.partial(step_kernel, n_cls, n_rep), out_shape=tu...  28.2 us
    pallas_call x1, Pallas kernels, per_device(): pl.pallas_call(pass_on, out_shape=tuple((jax.ShapeDtypeStruct(*out) for o...  0.85 us

profile of v2, /device:TPU:0, one launch (start us, length us, event | category | flops | bytes accessed | tf_op | source)
XLA Modules:
  0.0 30.4 jit_solution(15130125289924987848)
XLA Ops:
  1.3 28.2 %shard_map.112 = (f32[1,2]{1,0:T(1,128)S(1)}, bf16[1,2,768]{2,1,0:T(2,128)(2,1)S(1)}, bf16[384,768]{1,0:T(8,128)(2,1)S(1)}) custom-call(s32[1]{0:T(128)} %bitcast.3.slot_hbm, bf16[1,2,768]{2,1,0:T(2,128)(2,1)} %queries_hbm.1, s32[2,4,32]{2,1,0:T(4,128)} %bitcast.5, s32[32,1,384]{2,1,0:T(1,128)} %bitcast.4, f32[768]{0:T(1024)} %gain_hbm.1, ...), custom_call_target="tpu_custom_call" | custom-call | tf_op jit(solution)/shard_map/pallas_call | solution.py:448
  29.5 0.9 %shard_map.113 = (f32[1,2]{1,0:T(1,128)}, bf16[1,2,768]{2,1,0:T(2,128)(2,1)}, bf16[384,768]{1,0:T(8,128)(2,1)}) custom-call(f32[1,2]{1,0:T(1,128)S(1)} %get-tuple-element.6.refs_0_, bf16[1,2,768]{2,1,0:T(2,128)(2,1)S(1)} %get-tuple-element.7.refs_1_, bf16[384,768]{1,0:T(8,128)(2,1)S(1)} %get-tuple-element.8.refs_2_), custom_call_target="tpu_custom_call" | custom-call | tf_op jit(solution)/shard_map/pallas_call | solution.py:505

commit v3 on v2

--- a/solution.py
+++ b/solution.py
@@ -63,12 +63,15 @@
     targets_ref,
     gain_ref,
     labels,
+    turned_labels,
     features,
     weight,
     free,
     free_seats,
     seating,
     fresh_rows,
+    fresh_seen,
+    fresh_count,
     id_counts,
     q_slots,
     q_rows,
@@ -105,6 +108,12 @@
     lab_rows = usable * n_rep
     seats = n_cls * padded
     mine = rep * n_cls + cls
+    span = n_cls // PARTS
+    plane = cls // span
+    inner = (plane > 0) & (plane < PARTS - 1)
+
+    def seat_of(owner):
+        return (owner ^ cls) * padded
 
     barrier = pltpu.get_barrier_semaphore()
 
@@ -141,18 +150,24 @@
     rank = jnp.sum(jnp.where(t_col < t_row, 1.0, 0.0), axis=0, keepdims=True)
     owner = jnp.floor((rank + 0.5) * (1.0 / per_owner))
     seat_in = (rank - owner * per_owner).astype(jnp.int32)
-    place = (owner.astype(jnp.int32) ^ cls) * padded + seat_in
-    place_i = lax.broadcasted_iota(jnp.int32, (seats, half_rows), 0)
-    pick = jnp.where(place_i == place, 1.0, 0.0).astype(bf16)
+    place = seat_of(owner.astype(jnp.int32)) + seat_in
+    part_rows = span * padded
+
+    def encode(low, high):
+        rows = (high - low) * padded
+        place_i = low * padded + lax.broadcasted_iota(jnp.int32, (rows, half_rows), 0)
+        pick = jnp.where(place_i == place, 1.0, 0.0).astype(bf16)
+        ordered = jnp.dot(pick, features[...], preferred_element_type=f32).astype(bf16)
+        hidden = jnp.dot(ordered, weight[...], preferred_element_type=f32)
+        scale = lax.rsqrt(jnp.mean(hidden * hidden, axis=1, keepdims=True) + 1e-06)
+        encoded = hidden * scale * gain_ref[...].reshape(1, width)
+        for k in range(low, high):
+            out_rows[k] = encoded[(k - low) * padded : (k - low + 1) * padded].astype(bf16)
+
     loads[0].wait()
-    ordered = jnp.dot(pick, features[...], preferred_element_type=f32).astype(bf16)
     loads[2].wait()
-    hidden = jnp.dot(ordered, weight[...], preferred_element_type=f32)
-    scale = lax.rsqrt(jnp.mean(hidden * hidden, axis=1, keepdims=True) + 1e-06)
     loads[3].wait()
-    encoded = hidden * scale * gain_ref[...].reshape(1, width)
-    for k in range(n_cls):
-        out_rows[k] = encoded[k * padded : (k + 1) * padded].astype(bf16)
+    encode(n_cls // 2, n_cls)
     loads[4].wait()
 
     pl.semaphore_wait(barrier, n_cls)
@@ -166,13 +181,13 @@
             device_id=(cls ^ k, rep),
         )
 
-    def row_copy(k, slot, many, part):
+    def row_copy(slot, many, part):
         return pltpu.make_async_remote_copy(
             src_ref=out_rows.at[pl.ds(slot, many)],
             dst_ref=in_rows.at[pl.ds(slot, many)],
             send_sem=row_send,
             recv_sem=row_recv.at[part],
-            device_id=(cls ^ k, rep),
+            device_id=(cls ^ slot, rep),
         )
 
     def share_copy(k, source, slot, many):
@@ -184,13 +199,25 @@
             device_id=(cls ^ k, rep),
         )
 
-    each(n_cls - 1, lambda i: query_copy(n_cls - 1 - i, mine, 1).start())
-    query_copy(1, 0, n_cls - 1).wait_send()
-    span = n_cls // PARTS
-    for part in reversed(range(PARTS)):
+    def send_rows(part):
         top = (part + 1) * span - 1
-        count = span if part else span - 1
-        each(count, lambda i, top=top, part=part: row_copy(top - i, top - i, 1, part).start())
+        each(span if part else span - 1, lambda i: row_copy(top - i, 1, part).start())
+
+    each(n_cls - 1, lambda i: query_copy(i + 1, mine, 1).start())
+    pl.when(inner)(lambda: send_rows(2))
+    encode(0, n_cls // 2)
+
+    @pl.when(jnp.logical_not(inner))
+    def _():
+        query_copy(1, 0, n_cls - 1).wait_send()
+        for part in (3, 2, 1, 0):
+            send_rows(part)
+
+    @pl.when(inner)
+    def _():
+        for part in (1, 0, 3):
+            send_rows(part)
+
     in_rows[0] = out_rows[0]
 
     my_base = cls * slot_rows + rep * half_rows
@@ -205,7 +232,7 @@
     src_row = to_row(src_col, eye)
     before = jnp.where((src_col == src_row) & (col_i < row_i), 1.0, 0.0)
     count_col = jnp.sum(before, axis=1, keepdims=True)
-    seat_col = (src_col.astype(jnp.int32) ^ cls) * padded + count_col.astype(jnp.int32)
+    seat_col = seat_of(src_col.astype(jnp.int32)) + count_col.astype(jnp.int32)
     seat_row = to_row(seat_col.astype(f32), eye).astype(jnp.int32)
     seat_i = lax.broadcasted_iota(jnp.int32, (half_rows, seats), 1)
     seating[...] = jnp.where(seat_i == seat_col, 1.0, 0.0).astype(bf16)
@@ -234,17 +261,19 @@
             count = count + jnp.where(ids[p] == label, 1.0, 0.0)
         return count
 
-    part_rows = span * padded
     fresh_base = cls * lab_rows + slot_start + rep * half_rows
-    fresh_seen, fresh_count = [], []
     for part in range(PARTS):
         at_i = part * part_rows + lax.broadcasted_iota(jnp.int32, (half_rows, part_rows), 1)
         row_f = lax.broadcasted_iota(jnp.int32, (half_rows, part_rows), 0).astype(f32)
         at_row = jnp.sum(jnp.where(at_i == seat_col, row_f + 1.0, 0.0), axis=0, keepdims=True)
+        fresh_seen[part] = at_row
         at_row = at_row.astype(jnp.int32)
-        fresh_seen.append(at_row > 0)
-        fresh_count.append(counts_of(jnp.where(at_row > 0, fresh_base - 1 + at_row, -2)))
-
+        fresh_count[part] = counts_of(jnp.where(at_row > 0, fresh_base - 1 + at_row, -2))
+
+    for k in range(chunks):
+        loads[8 + k].wait()
+        at = slice(k * slot_rows, (k + 1) * slot_rows)
+        turned_labels[:, at] = labels[at].T
     query_copy(1, 0, n_cls - 1).wait_recv()
     side = q_slots.at[pl.ds(rep * n_cls, n_cls)]
     relay = pltpu.make_async_remote_copy(
@@ -272,9 +301,8 @@
     n = n_query
     peak = jnp.full((n, 1), NEG, f32)
     for k in range(chunks):
-        loads[8 + k].wait()
         at = slice(k * slot_rows, (k + 1) * slot_rows)
-        block = lax.dot_general(q, labels[at], NT, preferred_element_type=f32)
+        block = jnp.dot(q, turned_labels[:, at], preferred_element_type=f32)
         fresh = slot_start == rep * usable + k * slot_rows
         block = jnp.where(fresh, NEG, block)
         logits[:, at] = block
@@ -298,15 +326,16 @@
         grad = grad + (out[0:n] + out[n : 2 * n])
         hits, exp_sum, pos_sum = hits + out[2 * n : 3 * n], exp_sum + e, pos_sum + s
 
-    for part in [PARTS - 1, *range(PARTS - 1)]:
-        low = part * span if part else 1
-        row_copy(1, low, (part + 1) * span - low, part).wait_recv()
-        at = slice(part * part_rows, (part + 1) * part_rows)
-        landed = [in_rows[k].astype(f32) for k in range(part * span, (part + 1) * span)]
+    second = jnp.where(inner, 2, 1)
+    for turn, part in enumerate((0, second, jnp.where(inner, 1, 3), jnp.where(inner, 3, 2))):
+        low = part * span + (0 if turn else 1)
+        row_copy(low, span if turn else span - 1, part).wait_recv()
+        at = pl.ds(pl.multiple_of(part * part_rows, 16), part_rows)
+        landed = [in_rows[part * span + k].astype(f32) for k in range(span)]
         vectors = (free_seats[at] + jnp.concatenate(landed, axis=0)).astype(bf16)
         fresh_rows[at] = vectors
         block = lax.dot_general(q, vectors, NT, preferred_element_type=f32)
-        block = jnp.where(fresh_seen[part], block, NEG)
+        block = jnp.where(fresh_seen[part] > 0.0, block, NEG)
         top = jnp.maximum(peak, jnp.max(block, axis=1, keepdims=True))
         power = jnp.exp(block - top)
         high, rest = split(power)
@@ -372,7 +401,8 @@
 
     refreshed = jnp.dot(seating[...], fresh_rows[...], preferred_element_type=f32)
     refreshed_ref[...] = refreshed.astype(bf16)
-    row_copy(1, 1, n_cls - 1, 0).wait_send()
+    pl.when(inner)(lambda: query_copy(1, 0, n_cls - 1).wait_send())
+    row_copy(1, n_cls - 1, 0).wait_send()
     relay.wait_send()
     for swap in swaps:
         swap.wait_send()
@@ -456,12 +486,15 @@
             pltpu.VMEM((total, 1, half_rows), jnp.int32),
             pltpu.VMEM((width,), f32),
             pltpu.VMEM((usable, width), bf16),
+            pltpu.VMEM((width, usable), bf16),
             pltpu.VMEM((half_rows, width), bf16),
             pltpu.VMEM((width, width), bf16),
             pltpu.VMEM((half_rows, width), bf16),
             pltpu.VMEM((n_cls * padded, width), f32),
             pltpu.VMEM((half_rows, n_cls * padded), bf16),
             pltpu.VMEM((n_cls * padded, width), bf16),
+            pltpu.VMEM((PARTS, 1, n_cls // PARTS * padded), f32),
+            pltpu.VMEM((PARTS, n_query, n_cls // PARTS * padded), f32),
             pltpu.VMEM((n_query, STATS), f32),
             pltpu.VMEM((total, query_rows, width), bf16),
             pltpu.VMEM((n_query, width), f32),

time: 30.7 us -> 29.4 us (0.958)
  Pallas kernels: 29.1 us -> 27.9 us
    pallas_call x1, Pallas kernels: 28.2 us -> 27 us  [per_device(): pl.pallas_call(functools.partial(step_kernel, n_cls, n_rep), out_shape=tu...]
where the time goes in v3:
time: 29.4 us; the launch traced here: 29.2 us
  Pallas kernels  27.9 us (95%)
  between operations  1.29 us (4%)
    pallas_call x1, Pallas kernels, per_device(): pl.pallas_call(functools.partial(step_kernel, n_cls, n_rep), out_shape=tu...  27 us
    pallas_call x1, Pallas kernels, per_device(): pl.pallas_call(pass_on, out_shape=tuple((jax.ShapeDtypeStruct(*out) for o...  0.85 us

profile of v3, /device:TPU:0, one launch (start us, length us, event | category | flops | bytes accessed | tf_op | source)
XLA Modules:
  0.0 29.2 jit_solution(7903394926058106142)
XLA Ops:
  1.3 27.0 %shard_map.112 = (f32[1,2]{1,0:T(1,128)S(1)}, bf16[1,2,768]{2,1,0:T(2,128)(2,1)S(1)}, bf16[384,768]{1,0:T(8,128)(2,1)S(1)}) custom-call(s32[1]{0:T(128)} %bitcast.3.slot_hbm, bf16[1,2,768]{2,1,0:T(2,128)(2,1)} %queries_hbm.1, s32[2,4,32]{2,1,0:T(4,128)} %bitcast.5, s32[32,1,384]{2,1,0:T(1,128)} %bitcast.4, f32[768]{0:T(1024)} %gain_hbm.1, ...), custom_call_target="tpu_custom_call" | custom-call | tf_op jit(solution)/shard_map/pallas_call | solution.py:478
  28.3 0.9 %shard_map.113 = (f32[1,2]{1,0:T(1,128)}, bf16[1,2,768]{2,1,0:T(2,128)(2,1)}, bf16[384,768]{1,0:T(8,128)(2,1)}) custom-call(f32[1,2]{1,0:T(1,128)S(1)} %get-tuple-element.6.refs_0_, bf16[1,2,768]{2,1,0:T(2,128)(2,1)S(1)} %get-tuple-element.7.refs_1_, bf16[384,768]{1,0:T(8,128)(2,1)S(1)} %get-tuple-element.8.refs_2_), custom_call_target="tpu_custom_call" | custom-call | tf_op jit(solution)/shard_map/pallas_call | solution.py:538

commit v4 on v3

--- a/solution.py
+++ b/solution.py
@@ -11,6 +11,7 @@
 NEG = -1e30
 STATS = 128
 PARTS = 4
+PIECES = 8
 NT = (((1,), (1,)), ((), ()))
 
 
@@ -134,9 +135,8 @@
         (positives_hbm, positives_ref),
         (free_hbm, free),
     ]
-    for k in range(chunks):
-        start = pl.multiple_of(rep * usable + k * slot_rows, slot_rows)
-        pairs.append((labels_hbm.at[pl.ds(start, slot_rows)], labels.at[pl.ds(k * slot_rows, slot_rows)]))
+    start = pl.multiple_of(rep * usable, slot_rows)
+    pairs.append((labels_hbm.at[pl.ds(start, usable)], labels))
     loads = [pltpu.make_async_copy(a, b, load_sem.at[i]) for i, (a, b) in enumerate(pairs)]
     for copy in loads:
         copy.start()
@@ -270,8 +270,8 @@
         at_row = at_row.astype(jnp.int32)
         fresh_count[part] = counts_of(jnp.where(at_row > 0, fresh_base - 1 + at_row, -2))
 
+    loads[8].wait()
     for k in range(chunks):
-        loads[8 + k].wait()
         at = slice(k * slot_rows, (k + 1) * slot_rows)
         turned_labels[:, at] = labels[at].T
     query_copy(1, 0, n_cls - 1).wait_recv()
@@ -393,8 +393,8 @@
         shares_out[c, :, 2 * width :] = stats[at]
 
     def send_share(i):
-        k = n_cls - 1 - i
-        share_copy(k, cls ^ k, k, 1).start()
+        other = i + (cls <= i).astype(jnp.int32)
+        share_copy(cls ^ other, other, cls ^ other, 1).start()
 
     each(n_cls - 1, send_share)
     shares_in[0] = shares_out[cls]
@@ -429,16 +429,20 @@
     share_copy(1, 0, 1, n_cls - 1).wait_send()
 
 
-def pass_on(*refs):
-    sem = refs[-1]
-    half = len(refs) // 2
-    copies = []
-    for i, (source, target) in enumerate(zip(refs[:half], refs[half:-1])):
-        copy = pltpu.make_async_copy(source, target, sem.at[i])
+def pass_on(loss, grads, refreshed, loss_hbm, grads_hbm, refreshed_hbm, sem):
+    rows = refreshed.shape[0] // PIECES
+    for i in range(PIECES):
+        at = pl.ds(i * rows, rows)
+        pltpu.make_async_copy(refreshed.at[at], refreshed_hbm.at[at], sem.at[2]).start()
+    small = [
+        pltpu.make_async_copy(loss, loss_hbm, sem.at[0]),
+        pltpu.make_async_copy(grads, grads_hbm, sem.at[1]),
+    ]
+    for copy in small:
         copy.start()
-        copies.append(copy)
-    for copy in copies:
+    for copy in small:
         copy.wait()
+    pltpu.make_async_copy(refreshed, refreshed_hbm, sem.at[2]).wait()
 
 
 def per_device(
@@ -508,7 +512,7 @@
             pltpu.VMEM((own_half, width), bf16),
             pltpu.VMEM((n_cls, query_rows, share), bf16),
             pltpu.VMEM((n_cls, query_rows, share), bf16),
-            dma((8 + usable // slot_rows,)),
+            dma((9,)),
             dma((2,)),
             dma((2,)),
             dma,

time: 29.4 us -> 29 us (0.986)
  Pallas kernels: 27.9 us -> 27.6 us
    pallas_call x1, Pallas kernels: 27 us -> 26.7 us  [per_device(): pl.pallas_call(functools.partial(step_kernel, n_cls, n_rep), out_shape=tu...]
where the time goes in v4:
time: 29 us; the launch traced here: 28.8 us
  Pallas kernels  27.6 us (95%)
  between operations  1.29 us (4%)
    pallas_call x1, Pallas kernels, per_device(): pl.pallas_call(functools.partial(step_kernel, n_cls, n_rep), out_shape=tu...  26.7 us
    pallas_call x1, Pallas kernels, per_device(): pl.pallas_call(pass_on, out_shape=tuple((jax.ShapeDtypeStruct(*out) for o...  0.83 us

profile of v4, /device:TPU:0, one launch (start us, length us, event | category | flops | bytes accessed | tf_op | source)
XLA Modules:
  0.0 28.8 jit_solution(12559056149828739677)
XLA Ops:
  1.3 26.7 %shard_map.112 = (f32[1,2]{1,0:T(1,128)S(1)}, bf16[1,2,768]{2,1,0:T(2,128)(2,1)S(1)}, bf16[384,768]{1,0:T(8,128)(2,1)S(1)}) custom-call(s32[1]{0:T(128)} %bitcast.3.slot_hbm, bf16[1,2,768]{2,1,0:T(2,128)(2,1)} %queries_hbm.1, s32[2,4,32]{2,1,0:T(4,128)} %bitcast.5, s32[32,1,384]{2,1,0:T(1,128)} %bitcast.4, f32[768]{0:T(1024)} %gain_hbm.1, ...), custom_call_target="tpu_custom_call" | custom-call | tf_op jit(solution)/shard_map/pallas_call | solution.py:482
  28.0 0.8 %shard_map.113 = (f32[1,2]{1,0:T(1,128)}, bf16[1,2,768]{2,1,0:T(2,128)(2,1)}, bf16[384,768]{1,0:T(8,128)(2,1)}) custom-call(f32[1,2]{1,0:T(1,128)S(1)} %get-tuple-element.6.loss, bf16[1,2,768]{2,1,0:T(2,128)(2,1)S(1)} %get-tuple-element.7.grads, bf16[384,768]{1,0:T(8,128)(2,1)S(1)} %get-tuple-element.8.refreshed), custom_call_target="tpu_custom_call" | custom-call | tf_op jit(solution)/shard_map/pallas_call | solution.py:542

commit v5 on v4

--- a/solution.py
+++ b/solution.py
@@ -368,18 +368,26 @@
         swap.start()
         swaps.append(swap)
     x, xh = half_out[rep], hits_out[rep].astype(f32)
-    some = id_counts[pl.ds(pl.multiple_of(rep * own_half, own_half), own_half), :][:, 0:1]
+    some = id_counts[pl.ds(pl.multiple_of(rep * own_half, own_half), own_half), :]
     for swap in swaps:
         swap.wait_recv()
     y, yh = half_in[...], hits_in[...].astype(f32)
-    xs, ys = x[:, width:], y[:, width:]
-    m = jnp.maximum(xs[:, 0:1], ys[:, 0:1])
-    a, b = jnp.exp(xs[:, 0:1] - m), jnp.exp(ys[:, 0:1] - m)
-    exp_sum = xs[:, 1:2] * a + ys[:, 1:2] * b
-    pos_sum = xs[:, 2:3] + ys[:, 2:3]
+    tiles = width // STATS
+
+    def wide(v):
+        return jnp.concatenate([v] * tiles, axis=1)
+
+    def spread(v, i):
+        return jnp.broadcast_to(v[:, width + i : width + i + 1], some.shape)
+
+    xm, ym = spread(x, 0), spread(y, 0)
+    m = jnp.maximum(xm, ym)
+    a, b = jnp.exp(xm - m), jnp.exp(ym - m)
+    exp_sum = spread(x, 1) * a + spread(y, 1) * b
+    pos_sum = spread(x, 2) + spread(y, 2)
     hits = xh + yh
     inv = 1.0 / exp_sum
-    term = x[:, 0:width] * (a * inv) + y[:, 0:width] * (b * inv) - hits * (1.0 / some)
+    term = x[:, 0:width] * wide(a * inv) + y[:, 0:width] * wide(b * inv) - hits * wide(1.0 / some)
     lane = lax.broadcasted_iota(jnp.int32, (own_half, STATS), 1)
     stats = jnp.zeros((own_half, STATS), f32)
     for i, value in enumerate([m, exp_sum, pos_sum]):
@@ -409,21 +417,26 @@
     id_count = id_counts[pl.ds(mine * query_rows, query_rows), :][:, 0:1]
 
     share_copy(1, 0, 1, n_cls - 1).wait_recv()
-    stats = shares_in[:, :, 2 * width :].astype(f32)
-    stats = stats[:, :, 0:3] + stats[:, :, 3:6] + stats[:, :, 6:9]
-    ms, es = stats[:, :, 0:1], stats[:, :, 1:2]
-    pos_sum = jnp.sum(stats[:, :, 2:3], axis=0)
-    m = jnp.max(ms, axis=0)
-    es = es * jnp.exp(ms - m[None])
-    exp_sum = jnp.sum(es, axis=0)
-    rho = es * (1.0 / exp_sum)[None]
-    inv = 1.0 / id_count
-    back = (rho - 1.0) * inv[None]
+    stats = jnp.concatenate([shares_in[k, :, 2 * width :].astype(f32) for k in range(n_cls)], axis=0)
+
+    def gather(i):
+        parts = [jnp.broadcast_to(stats[:, 3 * j + i : 3 * j + i + 1], stats.shape) for j in range(3)]
+        whole = parts[0] + parts[1] + parts[2]
+        return [whole[k * query_rows : (k + 1) * query_rows] for k in range(n_cls)]
+
+    ms, es, ps = gather(0), gather(1), gather(2)
+    m = functools.reduce(jnp.maximum, ms)
+    es = [e * jnp.exp(x - m) for e, x in zip(es, ms)]
+    exp_sum = functools.reduce(jnp.add, es)
+    pos_sum = functools.reduce(jnp.add, ps)
+    inv, inv_count = 1.0 / exp_sum, 1.0 / id_count
     grad = jnp.zeros((query_rows, width), f32)
     for k in range(n_cls):
-        grad = grad + rho[k] * shares_in[k, :, 0:width].astype(f32)
-        grad = grad + back[k] * shares_in[k, :, width : 2 * width].astype(f32)
-    loss = m + jnp.log(exp_sum) - pos_sum / id_count
+        rho = es[k] * inv
+        back = (rho - 1.0) * inv_count
+        grad = grad + wide(rho) * shares_in[k, :, 0:width].astype(f32)
+        grad = grad + wide(back) * shares_in[k, :, width : 2 * width].astype(f32)
+    loss = (m + jnp.log(exp_sum))[:, 0:1] - pos_sum[:, 0:1] * inv_count
     loss_ref[...] = to_row(loss, eye_of(query_rows))
     grads_ref[0] = grad.astype(bf16)
     share_copy(1, 0, 1, n_cls - 1).wait_send()

time: 29 us -> 28.9 us (level)
  no operation moved by 1% of the time
where the time goes in v5:
time: 28.9 us; the launch traced here: 28.7 us
  Pallas kernels  27.4 us (95%)
  between operations  1.29 us (4%)
    pallas_call x1, Pallas kernels, per_device(): pl.pallas_call(functools.partial(step_kernel, n_cls, n_rep), out_shape=tu...  26.6 us
    pallas_call x1, Pallas kernels, per_device(): pl.pallas_call(pass_on, out_shape=tuple((jax.ShapeDtypeStruct(*out) for o...  0.83 us

profile of v5, /device:TPU:0, one launch (start us, length us, event | category | flops | bytes accessed | tf_op | source)
XLA Modules:
  0.0 28.7 jit_solution(4975988361825501370)
XLA Ops:
  1.3 26.6 %shard_map.112 = (f32[1,2]{1,0:T(1,128)S(1)}, bf16[1,2,768]{2,1,0:T(2,128)(2,1)S(1)}, bf16[384,768]{1,0:T(8,128)(2,1)S(1)}) custom-call(s32[1]{0:T(128)} %bitcast.3.slot_hbm, bf16[1,2,768]{2,1,0:T(2,128)(2,1)} %queries_hbm.1, s32[2,4,32]{2,1,0:T(4,128)} %bitcast.5, s32[32,1,384]{2,1,0:T(1,128)} %bitcast.4, f32[768]{0:T(1024)} %gain_hbm.1, ...), custom_call_target="tpu_custom_call" | custom-call | tf_op jit(solution)/shard_map/pallas_call | solution.py:495
  27.9 0.8 %shard_map.113 = (f32[1,2]{1,0:T(1,128)}, bf16[1,2,768]{2,1,0:T(2,128)(2,1)}, bf16[384,768]{1,0:T(8,128)(2,1)}) custom-call(f32[1,2]{1,0:T(1,128)S(1)} %get-tuple-element.6.loss, bf16[1,2,768]{2,1,0:T(2,128)(2,1)S(1)} %get-tuple-element.7.grads, bf16[384,768]{1,0:T(8,128)(2,1)S(1)} %get-tuple-element.8.refreshed), custom_call_target="tpu_custom_call" | custom-call | tf_op jit(solution)/shard_map/pallas_call | solution.py:555

commit v6 on v5

--- a/solution.py
+++ b/solution.py
@@ -351,15 +351,17 @@
 
     lane = lax.broadcasted_iota(jnp.int32, (n, STATS), 1)
     stats = jnp.where(lane == 0, peak, jnp.where(lane == 1, exp_sum, pos_sum))
-    for r in range(n_rep):
-        at = slice(r * own_half, (r + 1) * own_half)
-        half_out[r, :, 0:width] = grad[at]
-        half_out[r, :, width:] = stats[at]
-        hits_out[r] = hits[at].astype(bf16)
+
+    def half(v, r):
+        return jnp.where(r == 0, v[0:own_half], v[own_half:])
+
+    half_out[:, 0:width] = half(grad, partner)
+    half_out[:, width:] = half(stats, partner)
+    hits_out[...] = half(hits, partner).astype(bf16)
     swaps = []
     for i, (a, b) in enumerate([(half_out, half_in), (hits_out, hits_in)]):
         swap = pltpu.make_async_remote_copy(
-            src_ref=a.at[partner],
+            src_ref=a,
             dst_ref=b,
             send_sem=half_sem.at[i],
             recv_sem=half_sem.at[2 + i],
@@ -367,7 +369,8 @@
         )
         swap.start()
         swaps.append(swap)
-    x, xh = half_out[rep], hits_out[rep].astype(f32)
+    x = jnp.concatenate([half(grad, rep), half(stats, rep)], axis=1)
+    xh = half(hits, rep)
     some = id_counts[pl.ds(pl.multiple_of(rep * own_half, own_half), own_half), :]
     for swap in swaps:
         swap.wait_recv()
@@ -519,9 +522,9 @@
             pltpu.VMEM((n_cls, padded, width), bf16),
             pltpu.VMEM((n_query, usable), f32),
             pltpu.VMEM((3 * n_query, slot_rows), bf16),
-            pltpu.VMEM((n_rep, own_half, width + STATS), f32),
             pltpu.VMEM((own_half, width + STATS), f32),
-            pltpu.VMEM((n_rep, own_half, width), bf16),
+            pltpu.VMEM((own_half, width + STATS), f32),
+            pltpu.VMEM((own_half, width), bf16),
             pltpu.VMEM((own_half, width), bf16),
             pltpu.VMEM((n_cls, query_rows, share), bf16),
             pltpu.VMEM((n_cls, query_rows, share), bf16),

time: 28.9 us -> 28.9 us (level)
  no operation moved by 1% of the time
where the time goes in v6:
time: 28.9 us; the launch traced here: 28.7 us
  Pallas kernels  27.4 us (95%)
  between operations  1.29 us (4%)
    pallas_call x1, Pallas kernels, per_device(): pl.pallas_call(functools.partial(step_kernel, n_cls, n_rep), out_shape=tu...  26.6 us
    pallas_call x1, Pallas kernels, per_device(): pl.pallas_call(pass_on, out_shape=tuple((jax.ShapeDtypeStruct(*out) for o...  0.83 us

profile of v6, /device:TPU:0, one launch (start us, length us, event | category | flops | bytes accessed | tf_op | source)
XLA Modules:
  0.0 28.7 jit_solution(11959376808327412095)
XLA Ops:
  1.3 26.6 %shard_map.112 = (f32[1,2]{1,0:T(1,128)S(1)}, bf16[1,2,768]{2,1,0:T(2,128)(2,1)S(1)}, bf16[384,768]{1,0:T(8,128)(2,1)S(1)}) custom-call(s32[1]{0:T(128)} %bitcast.3.slot_hbm, bf16[1,2,768]{2,1,0:T(2,128)(2,1)} %queries_hbm.1, s32[2,4,32]{2,1,0:T(4,128)} %bitcast.5, s32[32,1,384]{2,1,0:T(1,128)} %bitcast.4, f32[768]{0:T(1024)} %gain_hbm.1, ...), custom_call_target="tpu_custom_call" | custom-call | tf_op jit(solution)/shard_map/pallas_call | solution.py:498
  27.9 0.8 %shard_map.113 = (f32[1,2]{1,0:T(1,128)}, bf16[1,2,768]{2,1,0:T(2,128)(2,1)}, bf16[384,768]{1,0:T(8,128)(2,1)}) custom-call(f32[1,2]{1,0:T(1,128)S(1)} %get-tuple-element.6.loss, bf16[1,2,768]{2,1,0:T(2,128)(2,1)S(1)} %get-tuple-element.7.grads, bf16[384,768]{1,0:T(8,128)(2,1)S(1)} %get-tuple-element.8.refreshed), custom_call_target="tpu_custom_call" | custom-call | tf_op jit(solution)/shard_map/pallas_call | solution.py:558
